TPU v7x, 32 devices: a whole 2x2x4 slice. The times are simulated.
32 devices in a mesh: wide: 8 (over y, x, core), narrow: 4 (over z).
Axes of the slice: x: 2, y: 2, z: 4, core: 2. Of those that a mesh axis runs over, the one named last changes fastest.
Arguments:
- tokens: bfloat16 [64, 512, 512], P(('wide', 'narrow')), may hold values from -6 to 6
- seg_ids: int32 [64, 512], P(('wide', 'narrow')), may hold values from 0 to 7, as said below
- positives: int32 [256], replicated, may hold values from 0 to 63
- norm1_gain: bfloat16 [512], replicated, may hold values from 0.5 to 1.5
- w_query: bfloat16 [512, 512], replicated, may hold values from -0.0625 to 0.0625
- w_key: bfloat16 [512, 512], replicated, may hold values from -0.25 to 0.25
- w_value: bfloat16 [512, 512], replicated, may hold values from -0.25 to 0.25
- w_attn_out: bfloat16 [512, 512], replicated, may hold values from -1 to 1
- rel_bias: bfloat16 [32, 8], replicated, may hold values from -4 to 4
- norm2_gain: bfloat16 [512], replicated, may hold values from 0.5 to 1.5
- w_in: bfloat16 [512, 2048], replicated, may hold values from -0.25 to 0.25
- w_ffn_out: bfloat16 [2048, 512], replicated, may hold values from -0.1875 to 0.1875
- w_proj: bfloat16 [512, 512], replicated, may hold values from -0.25 to 0.25
Outputs:
- loss: float32 [], replicated
- tokens_grad: bfloat16 [64, 512, 512], P(('wide', 'narrow'))
- norm1_gain_grad: float32 [512], replicated
- w_query_grad: float32 [512, 512], replicated
- w_key_grad: float32 [512, 512], replicated
- w_value_grad: float32 [512, 512], replicated
- w_attn_out_grad: float32 [512, 512], replicated
- rel_bias_grad: float32 [32, 8], replicated
- norm2_gain_grad: float32 [512], replicated
- w_in_grad: float32 [512, 2048], replicated
- w_ffn_out_grad: float32 [2048, 512], replicated
- w_proj_grad: float32 [512, 512], replicated
Inputs may be any that keep to these rules, and one draw needn't show every extreme that they name: `seg_ids`: each row of the first half holds 8 queries of 64 tokens, numbered 0 to 7 in order. Each row of the second half holds passage 0 and then passage 1, each of 64 to 448 tokens; the first such row has a passage 0 of exactly 448 tokens. `positives`: passages are numbered by row of the second half and then by their number within the row.
All inputs are finite; a program needn't handle non-finite values.
Results may differ from a plain program's by a relative error of at most 0.04.
The roundings to bfloat16 on the way count: a program that leaves them out, or rounds other values in their place, can miss the bound.
Values may be sent and summed in bfloat16 or wider, within the bound.
No kernel may reach another device: no remote copies, remote signals or barrier semaphores. Data moves between devices by JAX's collectives and lax.ppermute only.
A program may use at most 192 MiB of HBM per device.

v0:
```python
import jax
import jax.numpy as jnp
import numpy as np
from jax import lax
from jax.sharding import PartitionSpec as P

NB = 32
MAXD = 128
QLEN = 64
PPR = 2
EPS_NORM = 1e-06
LOGIT_SCALE = 50.0
MASKED = -1e30
HIGHEST = lax.Precision.HIGHEST
F32 = jnp.float32
BF16 = jnp.bfloat16


def bucket_offsets(length):
    offset = np.arange(-(length - 1), length)
    half_count = NB // 2
    exact_span = half_count // 2
    distance = -offset
    bucket = (distance < 0).astype(np.int64) * half_count
    distance = np.abs(distance)
    far_bucket = exact_span + (
        np.log(np.maximum(distance, 1) / exact_span)
        / np.log(MAXD / exact_span)
        * (half_count - exact_span)
    ).astype(np.int64)
    far_bucket = np.minimum(far_bucket, half_count - 1)
    bucket = bucket + np.where(distance < exact_span, distance, far_bucket)
    return bucket.astype(np.int32)


def toeplitz_rows(values, length):
    lead_shape = values.shape[:-1]
    tiled_values = jnp.tile(values, (1,) * len(lead_shape) + (length + 1,))
    start_at = length - 1
    window = tiled_values[..., start_at : start_at + length * (2 * length - 2)]
    return window.reshape(lead_shape + (length, 2 * length - 2))[..., :length]


def contract(left, right, left_dim, right_dim):
    return lax.dot_general(
        left, right, (((left_dim,), (right_dim,)), ((), ())), preferred_element_type=F32
    )


def rms_scale(values):
    return lax.rsqrt(jnp.mean(values * values, axis=-1, keepdims=True) + EPS_NORM)


def norm_back(grad_normed, inputs, scale, gain):
    scaled = grad_normed * gain
    return scale * scaled - inputs * scale**3 * jnp.mean(inputs * scaled, axis=-1, keepdims=True)


def score_block(queries, keys_rows, bias_full, same_seg):
    scores = jnp.einsum("ihd,jhd->hij", queries, keys_rows, preferred_element_type=F32) + bias_full
    return jnp.where(same_seg[None], scores, MASKED)


def local(
    tokens,
    seg_ids,
    positives,
    norm1_gain,
    w_query,
    w_key,
    w_value,
    w_attn_out,
    rel_bias,
    norm2_gain,
    w_in,
    w_ffn_out,
    w_proj,
):
    row_count, length, model_width = tokens.shape
    bucket_count, head_count = rel_bias.shape
    head_size = model_width // head_count
    slot_count = length // QLEN
    linear = lax.axis_index("wide") * lax.axis_size("narrow") + lax.axis_index("narrow")
    is_query = lax.axis_index("wide") < lax.axis_size("wide") // 2
    query_flag = is_query.astype(F32)
    gain_one = norm1_gain.astype(F32)
    gain_two = norm2_gain.astype(F32)
    offset_table = jnp.asarray(bucket_offsets(length))
    bucket_ids = jnp.arange(bucket_count, dtype=jnp.int32)
    offset_onehot = (offset_table[:, None] == bucket_ids[None, :]).astype(F32)
    offset_bias = jnp.dot(offset_onehot, rel_bias.astype(F32), precision=HIGHEST).T
    bias_full = toeplitz_rows(offset_bias, length)
    slot_ids = jnp.arange(slot_count, dtype=jnp.int32)
    stored = []
    embedded_rows = []
    for row_index in range(row_count):
        row_input = tokens[row_index].astype(F32)
        seg_row = seg_ids[row_index]
        scale_one = rms_scale(row_input)
        normed_one = (row_input * scale_one * gain_one).astype(BF16)
        queries = (
            jnp.dot(normed_one, w_query, preferred_element_type=F32)
            .astype(BF16)
            .reshape(length, head_count, head_size)
        )
        keys_rows = (
            jnp.dot(normed_one, w_key, preferred_element_type=F32)
            .astype(BF16)
            .reshape(length, head_count, head_size)
        )
        values_rows = (
            jnp.dot(normed_one, w_value, preferred_element_type=F32)
            .astype(BF16)
            .reshape(length, head_count, head_size)
        )
        same_seg = seg_row[:, None] == seg_row[None, :]
        scores = score_block(queries, keys_rows, bias_full, same_seg)
        row_top = jnp.max(scores, axis=-1, keepdims=True)
        exp_scores = jnp.exp(scores - row_top)
        row_total = jnp.sum(exp_scores, axis=-1, keepdims=True)
        attn_probs = exp_scores / row_total
        log_total = row_top + jnp.log(row_total)
        attn_mixed = jnp.einsum(
            "hij,jhd->ihd", attn_probs.astype(BF16), values_rows, preferred_element_type=F32
        )
        attn_mixed = attn_mixed.reshape(length, model_width).astype(BF16)
        hidden = row_input + jnp.dot(attn_mixed, w_attn_out, preferred_element_type=F32)
        scale_two = rms_scale(hidden)
        normed_two = (hidden * scale_two * gain_two).astype(BF16)
        ffn_inner = jnp.dot(normed_two, w_in, preferred_element_type=F32)
        active = jnp.where(ffn_inner > 0, ffn_inner, 0.0).astype(BF16)
        output = hidden + jnp.dot(active, w_ffn_out, preferred_element_type=F32)
        slot_mask = (seg_row[None, :] == slot_ids[:, None]).astype(F32)
        counts = jnp.maximum(jnp.sum(slot_mask, axis=-1, keepdims=True), 1.0)
        pooled = (jnp.dot(slot_mask, output, precision=HIGHEST) / counts).astype(BF16)
        projected = jnp.dot(pooled, w_proj, preferred_element_type=F32)
        inv_norm = lax.rsqrt(jnp.sum(projected * projected, axis=-1, keepdims=True) + EPS_NORM)
        embedded_rows.append((projected * inv_norm).astype(BF16))
        stored.append(
            (
                row_input,
                same_seg,
                scale_one,
                normed_one,
                queries,
                keys_rows,
                values_rows,
                log_total,
                attn_mixed,
                hidden,
                scale_two,
                normed_two,
                ffn_inner,
                active,
                slot_mask,
                counts,
                pooled,
                projected,
                inv_norm,
            )
        )
    emb_local = jnp.concatenate(embedded_rows, axis=0)
    own_count = row_count * slot_count
    gathered = lax.all_gather(emb_local, ("wide", "narrow"), axis=0, tiled=True)
    half_rows = gathered.shape[0] // (2 * slot_count)
    proj_width = gathered.shape[1]
    passage_all = (
        gathered[half_rows * slot_count :]
        .reshape(half_rows, slot_count, proj_width)[:, :PPR]
        .reshape(half_rows * PPR, proj_width)
    )
    passage_count = half_rows * PPR
    query_start = linear * own_count
    passage_ids = jnp.arange(passage_count, dtype=jnp.int32)
    targets = lax.dynamic_slice_in_dim(positives, query_start, own_count)
    logits = LOGIT_SCALE * contract(emb_local, passage_all, 1, 1)
    row_top = jnp.max(logits, axis=-1, keepdims=True)
    loss_log_total = row_top + jnp.log(jnp.sum(jnp.exp(logits - row_top), axis=-1, keepdims=True))
    pos_hits = (targets[:, None] == passage_ids[None, :]).astype(F32)
    per_query = loss_log_total[:, 0] - jnp.sum(logits * pos_hits, axis=-1)
    weights = (jnp.exp(logits - loss_log_total) - pos_hits).astype(BF16)
    per_query, weights = (per_query, weights)
    loss_part = query_flag * jnp.sum(per_query)
    query_grad = LOGIT_SCALE * jnp.dot(weights, passage_all, preferred_element_type=F32)
    passage_part = LOGIT_SCALE * query_flag * contract(weights, emb_local, 0, 0)
    operand = jnp.concatenate([jnp.zeros_like(passage_part), passage_part], axis=0)
    received = lax.psum_scatter(operand, ("wide", "narrow"), scatter_dimension=0, tiled=True)
    passage_slots = jnp.concatenate(
        [
            received.reshape(row_count, PPR, proj_width),
            jnp.zeros((row_count, slot_count - PPR, proj_width), F32),
        ],
        axis=1,
    ).reshape(own_count, proj_width)
    emb_grad = jnp.where(is_query, query_grad, passage_slots)
    grad_proj = jnp.zeros(w_proj.shape, F32)
    grad_ffn_out = jnp.zeros(w_ffn_out.shape, F32)
    grad_in = jnp.zeros(w_in.shape, F32)
    grad_gain_two = jnp.zeros((model_width,), F32)
    hidden_grads = []
    for row_index in range(row_count):
        (
            row_input,
            same_seg,
            scale_one,
            normed_one,
            queries,
            keys_rows,
            values_rows,
            log_total,
            attn_mixed,
            hidden,
            scale_two,
            normed_two,
            ffn_inner,
            active,
            slot_mask,
            counts,
            pooled,
            projected,
            inv_norm,
        ) = stored[row_index]
        emb_row_grad = emb_grad[row_index * slot_count : (row_index + 1) * slot_count]
        proj_grad = inv_norm * emb_row_grad - projected * inv_norm**3 * jnp.sum(
            emb_row_grad * projected, axis=-1, keepdims=True
        )
        proj_low = proj_grad.astype(BF16)
        grad_proj = grad_proj + contract(pooled, proj_low, 0, 0)
        pooled_grad = contract(proj_low, w_proj, 1, 1)
        out_grad = lax.dot_general(
            slot_mask, pooled_grad / counts, (((0,), (0,)), ((), ())), precision=HIGHEST
        )
        ffn_out_low = out_grad.astype(BF16)
        grad_ffn_out = grad_ffn_out + contract(active, ffn_out_low, 0, 0)
        active_grad = contract(ffn_out_low, w_ffn_out, 1, 1)
        inner_grad = jnp.where(ffn_inner > 0, active_grad, 0.0).astype(BF16)
        grad_in = grad_in + contract(normed_two, inner_grad, 0, 0)
        normed_two_grad = contract(inner_grad, w_in, 1, 1)
        grad_gain_two = grad_gain_two + jnp.sum(normed_two_grad * hidden * scale_two, axis=0)
        hidden_grads.append(out_grad + norm_back(normed_two_grad, hidden, scale_two, gain_two))
    grad_query = jnp.zeros(w_query.shape, F32)
    grad_key = jnp.zeros(w_key.shape, F32)
    grad_value = jnp.zeros(w_value.shape, F32)
    grad_attn_out = jnp.zeros(w_attn_out.shape, F32)
    score_grad_sum = jnp.zeros((head_count, length, length), F32)
    grad_gain_one = jnp.zeros((model_width,), F32)
    token_grads = []
    for row_index in range(row_count):
        (
            row_input,
            same_seg,
            scale_one,
            normed_one,
            queries,
            keys_rows,
            values_rows,
            log_total,
            attn_mixed,
            hidden,
            scale_two,
            normed_two,
            ffn_inner,
            active,
            slot_mask,
            counts,
            pooled,
            projected,
            inv_norm,
        ) = stored[row_index]
        hidden_grad = hidden_grads[row_index]
        attn_low = hidden_grad.astype(BF16)
        grad_attn_out = grad_attn_out + contract(attn_mixed, attn_low, 0, 0)
        mixed_grad = (
            contract(attn_low, w_attn_out, 1, 1).astype(BF16).reshape(length, head_count, head_size)
        )
        attn_probs = jnp.exp(score_block(queries, keys_rows, bias_full, same_seg) - log_total)
        values_grad = (
            jnp.einsum(
                "hij,ihd->jhd", attn_probs.astype(BF16), mixed_grad, preferred_element_type=F32
            )
            .astype(BF16)
            .reshape(length, model_width)
        )
        probs_grad = jnp.einsum("ihd,jhd->hij", mixed_grad, values_rows, preferred_element_type=F32)
        score_grad = (
            attn_probs * (probs_grad - jnp.sum(attn_probs * probs_grad, axis=-1, keepdims=True))
        ).astype(BF16)
        queries_grad = (
            jnp.einsum("hij,jhd->ihd", score_grad, keys_rows, preferred_element_type=F32)
            .astype(BF16)
            .reshape(length, model_width)
        )
        keys_grad = (
            jnp.einsum("hij,ihd->jhd", score_grad, queries, preferred_element_type=F32)
            .astype(BF16)
            .reshape(length, model_width)
        )
        score_grad_sum = score_grad_sum + score_grad.astype(F32)
        grad_query = grad_query + contract(normed_one, queries_grad, 0, 0)
        grad_key = grad_key + contract(normed_one, keys_grad, 0, 0)
        grad_value = grad_value + contract(normed_one, values_grad, 0, 0)
        normed_one_grad = (
            contract(queries_grad, w_query, 1, 1)
            + contract(keys_grad, w_key, 1, 1)
            + contract(values_grad, w_value, 1, 1)
        )
        grad_gain_one = grad_gain_one + jnp.sum(normed_one_grad * row_input * scale_one, axis=0)
        token_grads.append(
            (hidden_grad + norm_back(normed_one_grad, row_input, scale_one, gain_one)).astype(BF16)
        )
    pair_bucket = toeplitz_rows(offset_table[None, :], length)[0]
    pair_onehot = (bucket_ids[:, None] == pair_bucket.reshape(1, length * length)).astype(F32)
    grad_bias = lax.dot_general(
        score_grad_sum.reshape(head_count, length * length),
        pair_onehot,
        (((1,), (1,)), ((), ())),
        precision=HIGHEST,
    )
    sum_query, sum_key, sum_value, sum_attn_out, sum_in, sum_ffn_out, sum_proj = (
        lax.psum_scatter(
            grad_query.reshape(-1), ("wide", "narrow"), scatter_dimension=0, tiled=True
        ),
        lax.psum_scatter(grad_key.reshape(-1), ("wide", "narrow"), scatter_dimension=0, tiled=True),
        lax.psum_scatter(
            grad_value.reshape(-1), ("wide", "narrow"), scatter_dimension=0, tiled=True
        ),
        lax.psum_scatter(
            grad_attn_out.reshape(-1), ("wide", "narrow"), scatter_dimension=0, tiled=True
        ),
        lax.psum_scatter(grad_in.reshape(-1), ("wide", "narrow"), scatter_dimension=0, tiled=True),
        lax.psum_scatter(
            grad_ffn_out.reshape(-1), ("wide", "narrow"), scatter_dimension=0, tiled=True
        ),
        lax.psum_scatter(
            grad_proj.reshape(-1), ("wide", "narrow"), scatter_dimension=0, tiled=True
        ),
    )
    total_query, total_key, total_value, total_attn_out, total_in, total_ffn_out, total_proj = (
        lax.all_gather(
            sum_query.astype(jnp.bfloat16), ("wide", "narrow"), axis=0, tiled=True
        ).astype(sum_query.dtype),
        lax.all_gather(sum_key.astype(jnp.bfloat16), ("wide", "narrow"), axis=0, tiled=True).astype(
            sum_key.dtype
        ),
        lax.all_gather(
            sum_value.astype(jnp.bfloat16), ("wide", "narrow"), axis=0, tiled=True
        ).astype(sum_value.dtype),
        lax.all_gather(
            sum_attn_out.astype(jnp.bfloat16), ("wide", "narrow"), axis=0, tiled=True
        ).astype(sum_attn_out.dtype),
        lax.all_gather(sum_in.astype(jnp.bfloat16), ("wide", "narrow"), axis=0, tiled=True).astype(
            sum_in.dtype
        ),
        lax.all_gather(
            sum_ffn_out.astype(jnp.bfloat16), ("wide", "narrow"), axis=0, tiled=True
        ).astype(sum_ffn_out.dtype),
        lax.all_gather(
            sum_proj.astype(jnp.bfloat16), ("wide", "narrow"), axis=0, tiled=True
        ).astype(sum_proj.dtype),
    )
    loss_total, total_gain_one, total_gain_two, total_bias = lax.psum(
        (loss_part, grad_gain_one, grad_gain_two, grad_bias), ("wide", "narrow")
    )
    tokens_grad = jnp.stack(token_grads, axis=0)
    return (
        loss_total,
        tokens_grad,
        total_gain_one,
        total_query.reshape(w_query.shape),
        total_key.reshape(w_key.shape),
        total_value.reshape(w_value.shape),
        total_attn_out.reshape(w_attn_out.shape),
        total_bias.T,
        total_gain_two,
        total_in.reshape(w_in.shape),
        total_ffn_out.reshape(w_ffn_out.shape),
        total_proj.reshape(w_proj.shape),
    )


def solution(mesh):
    in_specs = (
        P(("wide", "narrow"), None, None),
        P(("wide", "narrow"), None),
        P(),
        P(),
        P(),
        P(),
        P(),
        P(),
        P(),
        P(),
        P(),
        P(),
        P(),
    )
    out_specs = (
        P(),
        P(("wide", "narrow"), None, None),
        P(),
        P(),
        P(),
        P(),
        P(),
        P(),
        P(),
        P(),
        P(),
        P(),
    )
    return jax.shard_map(local, mesh=mesh, in_specs=in_specs, out_specs=out_specs, check_vma=False)
```

profile of v0, /device:TPU:0, one launch (start us, length us, event | category | flops | bytes accessed | tf_op | source)
XLA Modules:
  0.0 1305.5 jit_solution(8156129899407925416)
XLA Ops:
  25.7 8.0 tile.8
  33.7 211.9 %while.1 = (u32[]{:T(128)}, f32[8,513,1023]{2,1,0:T(8,128)}, f32[4198392]{0:T(1024)}, u32[]{}, u32[]{}, /*index=5*/u32[]{}, u32[]{}) while((u32[]{:T(128)}, f32[8,513,1023]{2,1,0:T(8,128)}, f32[4198392]{0:T(1024)}, u32[]{}, u32[]{}, /*index=5*/u32[]{}, u32[]{}) %tuple.60), condition=%wide.cond, body=%wide.body.sunk | while | flops 9 | bytes 12595357
  37.4 4.2 reshape.518
  41.6 19.0 %dynamic-update-slice.2 = f32[4198392]{0:T(1024)} dynamic-update-slice(f32[4198392]{0:T(1024)} %get-tuple-element.177, f32[524799]{0:T(1024)} %reshape.518, u32[]{:T(128)S(6)} %add.320) | dynamic-update-slice | bytes 4198396
  63.8 4.2 reshape.518
  68.0 19.0 %dynamic-update-slice.2 = f32[4198392]{0:T(1024)} dynamic-update-slice(f32[4198392]{0:T(1024)} %get-tuple-element.177, f32[524799]{0:T(1024)} %reshape.518, u32[]{:T(128)S(6)} %add.320) | dynamic-update-slice | bytes 4198396
  90.2 4.2 reshape.518
  94.4 19.0 %dynamic-update-slice.2 = f32[4198392]{0:T(1024)} dynamic-update-slice(f32[4198392]{0:T(1024)} %get-tuple-element.177, f32[524799]{0:T(1024)} %reshape.518, u32[]{:T(128)S(6)} %add.320) | dynamic-update-slice | bytes 4198396
  116.6 4.2 reshape.518
  120.8 19.0 %dynamic-update-slice.2 = f32[4198392]{0:T(1024)} dynamic-update-slice(f32[4198392]{0:T(1024)} %get-tuple-element.177, f32[524799]{0:T(1024)} %reshape.518, u32[]{:T(128)S(6)} %add.320) | dynamic-update-slice | bytes 4198396
  143.0 4.2 reshape.518
  147.3 19.0 %dynamic-update-slice.2 = f32[4198392]{0:T(1024)} dynamic-update-slice(f32[4198392]{0:T(1024)} %get-tuple-element.177, f32[524799]{0:T(1024)} %reshape.518, u32[]{:T(128)S(6)} %add.320) | dynamic-update-slice | bytes 4198396
  169.5 4.2 reshape.518
  173.7 19.1 %dynamic-update-slice.2 = f32[4198392]{0:T(1024)} dynamic-update-slice(f32[4198392]{0:T(1024)} %get-tuple-element.177, f32[524799]{0:T(1024)} %reshape.518, u32[]{:T(128)S(6)} %add.320) | dynamic-update-slice | bytes 4198396
  196.0 4.2 reshape.518
  200.2 19.1 %dynamic-update-slice.2 = f32[4198392]{0:T(1024)} dynamic-update-slice(f32[4198392]{0:T(1024)} %get-tuple-element.177, f32[524799]{0:T(1024)} %reshape.518, u32[]{:T(128)S(6)} %add.320) | dynamic-update-slice | bytes 4198396
  222.5 4.2 reshape.518
  226.7 18.9 %dynamic-update-slice.2 = f32[4198392]{0:T(1024)} dynamic-update-slice(f32[4198392]{0:T(1024)} %get-tuple-element.177, f32[524799]{0:T(1024)} %reshape.518, u32[]{:T(128)S(6)} %add.320) | dynamic-update-slice | bytes 4198396
  245.6 20.6 %tile.18 = f32[8,524799]{1,0:T(8,128)} reshape(f32[4198392]{0:T(1024)} %get-tuple-element.64) | data formatting | bytes 33587136 | tf_op jit(solution)/shard_map/tile | solution.py:38
  266.2 12.9 slice.48
  279.0 13.9 %reshape.515 = f32[4186112]{0:T(1024)} reshape(f32[8,523264]{1,0:T(8,128)} %slice.48) | data formatting | bytes 33488896
  292.9 18.2 %reshape.451 = f32[8,512,1022]{2,1,0:T(8,128)} reshape(f32[4186112]{0:T(1024)} %reshape.515) | data formatting | bytes 33488896 | tf_op jit(solution)/shard_map/reshape | solution.py:41
  311.1 7.6 slice.49
  318.8 9.3 copy.147
  328.0 5.3 fusion.118
  357.9 73.9 %all_gather.24 = bf16[512,512]{1,0:T(8,128)(2,1)S(1)} all-gather(bf16[16,512]{1,0:T(8,128)(2,1)S(1)} %pad_maximum_fusion.1), channel_id=1, replica_groups=mesh['wide'=8,'narrow'=4] {'wide','narrow'}, dimensions={0}, use_global_device_ids=true | all-gather | bytes 540672 | tf_op jit(solution)/shard_map/all_gather | solution.py:164
  435.8 6.2 tile.20
  442.0 24.4 %slice_reduce_fusion = s32[523264]{0:T(1024)} fusion(s32[1,524799]{1,0:T(1,128)} %tile.20), kind=kLoop, calls=%fused_computation.36 | loop fusion | bytes 4186112 | tf_op jit(solution)/shard_map/slice | solution.py:40
  466.4 4.5 reshape.480
  474.1 83.0 %all-reduce.14.cloned.1.call-done = f32[128,512]{1,0:T(8,128)} async-done(((f32[128,512]{1,0:T(8,128)}), f32[128,512]{1,0:T(8,128)}) %all-reduce.14.cloned.1.call-update) | async-done | bytes 262160
  565.1 5.9 fusion.7
  578.6 4.4 fusion.9
  590.8 3.3 fusion.97
  597.0 5.1 multiply_reduce_fusion
  603.6 5.1 multiply_reduce_fusion.1
  608.7 18.7 %convert_add_fusion = (f32[8,512,512]{1,2,0:T(8,128)}, bf16[8,512,512]{1,2,0:T(8,128)(2,1)}, bf16[8,512,512]{1,2,0:T(8,128)(2,1)}) fusion(f32[8,512,512]{1,2,0:T(8,128)} %get-tuple-element.141, f32[8,512]{1,0:T(8,128)S(1)} %get-tuple-element.140, f32[8,512,512]{1,2,0:T(8,128)} %copy-done.2, f32[8,512]{1,0:T(8,128)S(1)} %get-tuple-element.147, ...), kind=kLoop, calls=%fused_computation.3 | loop fusion | flops 23068672 | bytes 50397184 | tf_op jit(solution)/shard_map/add | solution.py:298
  627.4 4.7 convolution_convert_fusion.2
  655.0 9.3 copy.124
  664.3 8.3 copy.154
  678.6 15.9 %fusion = f32[32,8]{0,1:T(8,128)S(1)} fusion(f32[8,262144]{1,0:T(8,128)S(1)} %bitcast.251, s32[262144]{0:T(1024)S(1)} %bitcast.285), kind=kOutput, calls=%fused_computation.1 | convolution fusion | flops 813694976 | bytes 9438208 | tf_op jit(solution)/shard_map/dot_general | solution.py:313
  696.3 230.0 %all-reduce.15 = (bf16[262144]{0:T(1024)(128)(2,1)}, bf16[262144]{0:T(1024)(128)(2,1)}, bf16[262144]{0:T(1024)(128)(2,1)}, bf16[262144]{0:T(1024)(128)(2,1)}, bf...) all-reduce(f32[262144]{0:T(1024)} %bitcast.272, ...), channel_id=3, replica_groups=mesh['wide'=8,'narrow'=4] {'wide','narrow'}, use_global_device_ids=true, to_apply=%region_29.30.clone | all-reduce | flops 3409153 | bytes 20457480
  936.6 70.3 %all_gather.25 = bf16[262144]{0:T(1024)(128)(2,1)S(1)} all-gather(bf16[8192]{0:T(1024)(128)(2,1)S(1)} %dynamic-slice.23), channel_id=1, replica_groups=mesh['wide'=8,'narrow'=4] {'wide','narrow'}, dimensions={0}, use_global_device_ids=true | all-gather | bytes 540672 | tf_op jit(solution)/shard_map/all_gather | solution.py:339
  1008.1 69.5 %all_gather.26 = bf16[262144]{0:T(1024)(128)(2,1)S(1)} all-gather(bf16[8192]{0:T(1024)(128)(2,1)S(1)} %dynamic-slice.22), channel_id=1, replica_groups=mesh['wide'=8,'narrow'=4] {'wide','narrow'}, dimensions={0}, use_global_device_ids=true | all-gather | bytes 540672 | tf_op jit(solution)/shard_map/all_gather | solution.py:342
  1078.9 69.3 %all_gather.27 = bf16[262144]{0:T(1024)(128)(2,1)S(1)} all-gather(bf16[8192]{0:T(1024)(128)(2,1)S(1)} %dynamic-slice.21), channel_id=1, replica_groups=mesh['wide'=8,'narrow'=4] {'wide','narrow'}, dimensions={0}, use_global_device_ids=true | all-gather | bytes 540672 | tf_op jit(solution)/shard_map/all_gather | solution.py:345
  1149.4 68.1 %all_gather.28 = bf16[262144]{0:T(1024)(128)(2,1)S(1)} all-gather(bf16[8192]{0:T(1024)(128)(2,1)S(1)} %dynamic-slice.20), channel_id=1, replica_groups=mesh['wide'=8,'narrow'=4] {'wide','narrow'}, dimensions={0}, use_global_device_ids=true | all-gather | bytes 540672 | tf_op jit(solution)/shard_map/all_gather | solution.py:348
  1218.8 69.2 %all_gather.31 = bf16[262144]{0:T(1024)(128)(2,1)S(1)} all-gather(bf16[8192]{0:T(1024)(128)(2,1)S(1)} %dynamic-slice.19), channel_id=1, replica_groups=mesh['wide'=8,'narrow'=4] {'wide','narrow'}, dimensions={0}, use_global_device_ids=true | all-gather | bytes 540672 | tf_op jit(solution)/shard_map/all_gather | solution.py:357
  1289.2 4.6 reshape.501
  1293.9 4.6 reshape.503
  (303 shorter events, 148.8 us)
Async XLA Ops:
  7.2 341.4 %copy-start = (bf16[512,2048]{1,0:T(8,128)(2,1)S(1)}, bf16[512,2048]{1,0:T(8,128)(2,1)}, u32[]{:S(2)}) copy-start(bf16[512,2048]{1,0:T(8,128)(2,1)} %param.24) | copy-start | bytes 6291460
  7.2 550.0 %all-reduce.14.cloned.1.call-start = ((), (), s32[]{:S(2)}) async-start(), calls=%async_computation.2 | async-start | bytes 524288
  10.2 13.9 %copy-start.61 = (f32[512]{0:T(512)}, f32[512]{0:T(512)S(1)}, u32[]{:S(2)}) copy-start(f32[512]{0:T(512)S(1)} %convert_element_type.250) | copy-start | bytes 6148
  13.2 10.8 copy-start.63
  14.5 5.5 copy-start.49
  14.5 6.9 copy-start.52
  14.6 8.0 copy-start.54
  15.2 8.8 copy-start.65
  20.0 5.4 copy-start.70
  20.0 5.4 copy-start.69
  20.0 5.4 copy-start.71
  333.3 3.9 copy-start.2
  333.3 3.9 copy-start.59
  334.6 4.8 slice-start.4
  337.2 3.9 slice-start.5
  337.2 3.9 copy-start.40
  337.2 3.9 copy-start.42
  338.8 4.1 copy-start.45
  339.3 15.6 %copy-start.11 = (f32[512,512]{0,1:T(8,128)}, f32[512,512]{0,1:T(8,128)S(1)}, u32[]{:S(2)}) copy-start(f32[512,512]{0,1:T(8,128)S(1)} %get-tuple-element.132) | copy-start | bytes 3145732
  355.0 77.3 %copy-start.72 = (s32[256]{0:T(256)S(1)}, s32[256]{0:T(256)}, u32[]{:S(2)}) copy-start(s32[256]{0:T(256)} %param.16) | copy-start | bytes 3076
  434.1 855.1 %all-gather.3.cloned.1.call-start = ((), (), s32[]{:S(2)}) async-start(), calls=%async_computation | async-start | bytes 2162688 | tf_op jit(solution)/shard_map/all_gather | solution.py:351
  565.1 5.9 copy-start.5
  565.1 5.9 copy-start.17
  583.1 4.7 copy-start.22
  587.9 6.9 slice-start
  590.3 4.4 slice-start.1
  594.8 7.3 slice-start.2
  597.0 5.1 slice-start.3
  603.6 49.2 %copy-start.27 = (bf16[8,64,512]{2,1,0:T(8,128)(2,1)}, bf16[8,64,512]{2,1,0:T(8,128)(2,1)S(1)}, u32[]{:S(2)}) copy-start(bf16[8,64,512]{2,1,0:T(8,128)(2,1)S(1)} %fusion.35) | copy-start | bytes 1572868
  627.4 4.8 copy-start.9
  627.4 4.8 copy-start.44
  627.4 6.4 copy-start.8
  627.4 6.4 copy-start.43
  632.2 3.8 copy-start.41
  636.0 3.7 copy-start.38
  636.0 5.3 copy-start.18
  636.8 4.5 copy-start.7
  636.9 4.5 copy-start.13
  642.7 4.9 copy-start.23
  649.8 3.5 copy-start.32
  664.3 8.4 copy-start.30
  664.3 8.9 copy-start.29
  678.5 16.0 %copy-start.19 = (f32[512,512]{0,1:T(8,128)}, f32[512,512]{0,1:T(8,128)S(1)}, u32[]{:S(2)}) copy-start(f32[512,512]{0,1:T(8,128)S(1)} %convolution_add_fusion.2) | copy-start | bytes 3145732
  678.6 16.0 %copy-start.33 = (bf16[8,64,512]{2,1,0:T(8,128)(2,1)S(1)}, bf16[8,64,512]{2,1,0:T(8,128)(2,1)}, u32[]{:S(2)}) copy-start(bf16[8,64,512]{2,1,0:T(8,128)(2,1)} %fusion.38) | copy-start | bytes 1572868
  696.3 233.1 %copy-start.67 = (f32[512]{0:T(512)S(1)}, f32[512]{0:T(512)}, u32[]{:S(2)}) copy-start(f32[512]{0:T(512)} %get-tuple-element.109) | copy-start | bytes 6148
  696.3 233.1 %copy-start.68 = (f32[512]{0:T(512)S(1)}, f32[512]{0:T(512)}, u32[]{:S(2)}) copy-start(f32[512]{0:T(512)} %get-tuple-element.107) | copy-start | bytes 6148
  927.9 366.0 %all-gather.5.cloned.1.call-start = ((), (), s32[]{:S(2)}) async-start(), calls=%async_computation.1 | async-start | bytes 2162688 | tf_op jit(solution)/shard_map/all_gather | solution.py:354
  1289.2 9.3 copy-start.1
  (34 other events, 80.1 us)
Sparse Core Ops, SparseCore 0:
  434.2 122.8 all-reduce.13
  928.0 55.0 all-gather.2
  986.0 55.6 all-gather.4
where the time goes:
time: 1320 us; the launch traced here: 1310 us
  blocking collectives  650 us (49%)
  local copies, waits for them, and re-layouts  417 us (32%)
  matrix products  110 us (8%)
  waiting for transfers between devices  83.1 us (6%)
  other arithmetic  28.6 us (2%)
  between operations  15.9 us (1%)
    unnamed x205, local copies, waits for them, and re-layouts  279 us
    unnamed x1, blocking collectives  230 us
    unnamed x4, waiting for transfers between devices  83.1 us
    all_gather x1, blocking collectives, local(): gathered = lax.all_gather(emb_local, ('wide', 'narrow'), axis=0, tiled=True)  73.9 us
    all_gather x1, blocking collectives, local(): lax.all_gather(sum_query.astype(jnp.bfloat16), ('wide', 'narrow'), axis=0...  70.3 us
    all_gather x1, blocking collectives, local(): lax.all_gather(sum_key.astype(jnp.bfloat16), ('wide', 'narrow'), axis=0,...  69.5 us
    all_gather x1, blocking collectives, local(): lax.all_gather(sum_value.astype(jnp.bfloat16), ('wide', 'narrow'), axis=0...  69.3 us
    all_gather x1, blocking collectives, local(): lax.all_gather(sum_proj.astype(jnp.bfloat16), ('wide', 'narrow'), axis=0,...  69.2 us
  transfers between devices with their start and end apart: 3, of which 1 were waited for; matrix products, arithmetic and copies ran while one was open for 5% of the time, Pallas kernels for 0%

commit v1 on v0

--- a/solution.py
+++ b/solution.py
@@ -1,3 +1,4 @@
+import functools
 import jax
 import jax.numpy as jnp
 import numpy as np
@@ -14,6 +15,16 @@
 HIGHEST = lax.Precision.HIGHEST
 F32 = jnp.float32
 BF16 = jnp.bfloat16
+
+
+def widths_create(matrix, d_out):
+    tmp = tuple((matrix for _ in range(lax.psum(1, ("wide", "narrow")))))
+    u_next = jnp.stack(tmp)
+    near = lax.all_to_all(u_next, ("wide", "narrow"), 0, 0)
+    return jnp.concatenate(near, axis=d_out)
+
+
+number_knots = functools.partial(widths_create, d_out=0)
 
 
 def bucket_offsets(length):
@@ -336,9 +347,7 @@
         ),
     )
     total_query, total_key, total_value, total_attn_out, total_in, total_ffn_out, total_proj = (
-        lax.all_gather(
-            sum_query.astype(jnp.bfloat16), ("wide", "narrow"), axis=0, tiled=True
-        ).astype(sum_query.dtype),
+        number_knots(sum_query.astype(jnp.bfloat16)).astype(sum_query.dtype),
         lax.all_gather(sum_key.astype(jnp.bfloat16), ("wide", "narrow"), axis=0, tiled=True).astype(
             sum_key.dtype
         ),

time: 1320 us -> 1280 us (0.970)
  blocking collectives: 650 us -> 592 us
    all_gather x1 -> x0, blocking collectives: 70.3 us -> none  [local(): lax.all_gather(sum_query.astype(jnp.bfloat16), ('wide', 'narrow'), axis=0...]
    unnamed x205 -> x207, local copies, waits for them, and re-layouts: 279 us -> 281 us
  transfers between devices with their start and end apart: 3 -> 4, of which waited for: 1 -> 1; matrix products, arithmetic and copies ran while one was open for 5% -> 5% of each run, Pallas kernels for 0% -> 0%
where the time goes in v1:
time: 1280 us; the launch traced here: 1260 us
  blocking collectives  592 us (46%)
  local copies, waits for them, and re-layouts  420 us (33%)
  matrix products  110 us (9%)
  waiting for transfers between devices  83.2 us (6%)
  other arithmetic  35.4 us (3%)
  between operations  15.7 us (1%)
    unnamed x207, local copies, waits for them, and re-layouts  281 us
    unnamed x1, blocking collectives  230 us
    unnamed x4, waiting for transfers between devices  83.2 us
    all_gather x1, blocking collectives, local(): lax.all_gather(sum_key.astype(jnp.bfloat16), ('wide', 'narrow'), axis=0,...  81.2 us
    all_gather x1, blocking collectives, local(): gathered = lax.all_gather(emb_local, ('wide', 'narrow'), axis=0, tiled=True)  73.9 us
    all_gather x1, blocking collectives, local(): lax.all_gather(sum_attn_out.astype(jnp.bfloat16), ('wide', 'narrow'), axi...  69.2 us
    all_gather x1, blocking collectives, local(): lax.all_gather(sum_proj.astype(jnp.bfloat16), ('wide', 'narrow'), axis=0,...  69 us
    all_gather x1, blocking collectives, local(): lax.all_gather(sum_value.astype(jnp.bfloat16), ('wide', 'narrow'), axis=0...  68.2 us
  transfers between devices with their start and end apart: 4, of which 1 were waited for; matrix products, arithmetic and copies ran while one was open for 5% of the time, Pallas kernels for 0%

profile of v1, /device:TPU:0, one launch (start us, length us, event | category | flops | bytes accessed | tf_op | source)
XLA Modules:
  0.0 1259.6 jit_solution(4184445287538813280)
XLA Ops:
  25.7 8.0 tile.8
  33.7 212.0 %while.1 = (u32[]{:T(128)}, f32[8,513,1023]{2,1,0:T(8,128)}, f32[4198392]{0:T(1024)}, u32[]{}, u32[]{}, /*index=5*/u32[]{}, u32[]{}) while((u32[]{:T(128)}, f32[8,513,1023]{2,1,0:T(8,128)}, f32[4198392]{0:T(1024)}, u32[]{}, u32[]{}, /*index=5*/u32[]{}, u32[]{}) %tuple.60), condition=%wide.cond, body=%wide.body.sunk | while | flops 9 | bytes 12595357
  37.4 4.2 reshape.525
  41.6 19.0 %dynamic-update-slice.2 = f32[4198392]{0:T(1024)} dynamic-update-slice(f32[4198392]{0:T(1024)} %get-tuple-element.177, f32[524799]{0:T(1024)} %reshape.525, u32[]{:T(128)S(6)} %add.322) | dynamic-update-slice | bytes 4198396
  63.8 4.2 reshape.525
  68.0 19.0 %dynamic-update-slice.2 = f32[4198392]{0:T(1024)} dynamic-update-slice(f32[4198392]{0:T(1024)} %get-tuple-element.177, f32[524799]{0:T(1024)} %reshape.525, u32[]{:T(128)S(6)} %add.322) | dynamic-update-slice | bytes 4198396
  90.2 4.2 reshape.525
  94.5 19.0 %dynamic-update-slice.2 = f32[4198392]{0:T(1024)} dynamic-update-slice(f32[4198392]{0:T(1024)} %get-tuple-element.177, f32[524799]{0:T(1024)} %reshape.525, u32[]{:T(128)S(6)} %add.322) | dynamic-update-slice | bytes 4198396
  116.6 4.2 reshape.525
  120.8 19.0 %dynamic-update-slice.2 = f32[4198392]{0:T(1024)} dynamic-update-slice(f32[4198392]{0:T(1024)} %get-tuple-element.177, f32[524799]{0:T(1024)} %reshape.525, u32[]{:T(128)S(6)} %add.322) | dynamic-update-slice | bytes 4198396
  143.1 4.2 reshape.525
  147.3 19.0 %dynamic-update-slice.2 = f32[4198392]{0:T(1024)} dynamic-update-slice(f32[4198392]{0:T(1024)} %get-tuple-element.177, f32[524799]{0:T(1024)} %reshape.525, u32[]{:T(128)S(6)} %add.322) | dynamic-update-slice | bytes 4198396
  169.5 4.2 reshape.525
  173.8 19.1 %dynamic-update-slice.2 = f32[4198392]{0:T(1024)} dynamic-update-slice(f32[4198392]{0:T(1024)} %get-tuple-element.177, f32[524799]{0:T(1024)} %reshape.525, u32[]{:T(128)S(6)} %add.322) | dynamic-update-slice | bytes 4198396
  196.0 4.2 reshape.525
  200.3 19.1 %dynamic-update-slice.2 = f32[4198392]{0:T(1024)} dynamic-update-slice(f32[4198392]{0:T(1024)} %get-tuple-element.177, f32[524799]{0:T(1024)} %reshape.525, u32[]{:T(128)S(6)} %add.322) | dynamic-update-slice | bytes 4198396
  222.5 4.2 reshape.525
  226.8 18.9 %dynamic-update-slice.2 = f32[4198392]{0:T(1024)} dynamic-update-slice(f32[4198392]{0:T(1024)} %get-tuple-element.177, f32[524799]{0:T(1024)} %reshape.525, u32[]{:T(128)S(6)} %add.322) | dynamic-update-slice | bytes 4198396
  245.7 20.6 %tile.18 = f32[8,524799]{1,0:T(8,128)} reshape(f32[4198392]{0:T(1024)} %get-tuple-element.64) | data formatting | bytes 33587136 | tf_op jit(solution)/shard_map/tile | solution.py:49
  266.2 12.9 %slice.48 = f32[8,523264]{1,0:T(8,128)} slice(f32[8,524799]{1,0:T(8,128)} %tile.18), slice={[0:8], [511:523775]} | slice | bytes 33488896 | tf_op jit(solution)/shard_map/slice | solution.py:51
  279.1 13.9 %reshape.520 = f32[4186112]{0:T(1024)} reshape(f32[8,523264]{1,0:T(8,128)} %slice.48) | data formatting | bytes 33488896
  293.0 18.2 %reshape.458 = f32[8,512,1022]{2,1,0:T(8,128)} reshape(f32[4186112]{0:T(1024)} %reshape.520) | data formatting | bytes 33488896 | tf_op jit(solution)/shard_map/reshape | solution.py:52
  311.2 7.6 slice.49
  318.8 9.3 copy.147
  328.1 5.3 fusion.118
  358.0 73.9 %all_gather.21 = bf16[512,512]{1,0:T(8,128)(2,1)S(1)} all-gather(bf16[16,512]{1,0:T(8,128)(2,1)S(1)} %pad_maximum_fusion.1), channel_id=1, replica_groups=mesh['wide'=8,'narrow'=4] {'wide','narrow'}, dimensions={0}, use_global_device_ids=true | all-gather | bytes 540672 | tf_op jit(solution)/shard_map/all_gather | solution.py:175
  435.8 6.2 tile.20
  442.1 24.4 %slice_reduce_fusion = s32[523264]{0:T(1024)} fusion(s32[1,524799]{1,0:T(1,128)} %tile.20), kind=kLoop, calls=%fused_computation.36 | loop fusion | bytes 4186112 | tf_op jit(solution)/shard_map/slice | solution.py:51
  466.4 4.5 reshape.485
  474.1 83.2 %all-reduce.14.cloned.1.call-done = f32[128,512]{1,0:T(8,128)} async-done(((f32[128,512]{1,0:T(8,128)}), f32[128,512]{1,0:T(8,128)}) %all-reduce.14.cloned.1.call-update) | async-done | bytes 262160
  565.2 5.9 fusion.7
  578.8 4.4 fusion.9
  590.9 3.3 fusion.97
  597.2 5.1 multiply_reduce_fusion
  603.7 5.1 multiply_reduce_fusion.1
  608.8 18.7 %convert_add_fusion = (f32[8,512,512]{1,2,0:T(8,128)}, bf16[8,512,512]{1,2,0:T(8,128)(2,1)}, bf16[8,512,512]{1,2,0:T(8,128)(2,1)}) fusion(f32[8,512,512]{1,2,0:T(8,128)} %get-tuple-element.141, f32[8,512]{1,0:T(8,128)S(1)} %get-tuple-element.140, f32[8,512,512]{1,2,0:T(8,128)} %copy-done.2, f32[8,512]{1,0:T(8,128)S(1)} %get-tuple-element.147, ...), kind=kLoop, calls=%fused_computation.3 | loop fusion | flops 23068672 | bytes 50397184 | tf_op jit(solution)/shard_map/add | solution.py:309
  627.6 4.7 convolution_convert_fusion.2
  655.1 9.3 copy.124
  664.5 8.3 copy.154
  678.7 15.9 %fusion = f32[32,8]{0,1:T(8,128)S(1)} fusion(f32[8,262144]{1,0:T(8,128)S(1)} %bitcast.251, s32[262144]{0:T(1024)S(1)} %bitcast.285), kind=kOutput, calls=%fused_computation.1 | convolution fusion | flops 813694976 | bytes 9438208 | tf_op jit(solution)/shard_map/dot_general | solution.py:324
  696.5 230.2 %all-reduce.15 = (bf16[262144]{0:T(1024)(128)(2,1)}, bf16[262144]{0:T(1024)(128)(2,1)}, bf16[262144]{0:T(1024)(128)(2,1)}, bf16[1048576]{0:T(1024)(128)(2,1)}, b...) all-reduce(f32[262144]{0:T(1024)} %bitcast.271, ...), channel_id=4, replica_groups=mesh['wide'=8,'narrow'=4] {'wide','narrow'}, use_global_device_ids=true, to_apply=%region_30.31.clone | all-reduce | flops 3409153 | bytes 20457480
  938.3 3.8 reduce.6
  946.2 81.2 %all_gather.22 = bf16[262144]{0:T(1024)(128)(2,1)S(1)} all-gather(bf16[8192]{0:T(1024)(128)(2,1)S(1)} %dynamic-slice.22), channel_id=1, replica_groups=mesh['wide'=8,'narrow'=4] {'wide','narrow'}, dimensions={0}, use_global_device_ids=true | all-gather | bytes 540672 | tf_op jit(solution)/shard_map/all_gather | solution.py:351
  1028.7 68.2 %all_gather.23 = bf16[262144]{0:T(1024)(128)(2,1)S(1)} all-gather(bf16[8192]{0:T(1024)(128)(2,1)S(1)} %dynamic-slice.21), channel_id=1, replica_groups=mesh['wide'=8,'narrow'=4] {'wide','narrow'}, dimensions={0}, use_global_device_ids=true | all-gather | bytes 540672 | tf_op jit(solution)/shard_map/all_gather | solution.py:354
  1098.1 69.2 %all_gather.24 = bf16[262144]{0:T(1024)(128)(2,1)S(1)} all-gather(bf16[8192]{0:T(1024)(128)(2,1)S(1)} %dynamic-slice.20), channel_id=1, replica_groups=mesh['wide'=8,'narrow'=4] {'wide','narrow'}, dimensions={0}, use_global_device_ids=true | all-gather | bytes 540672 | tf_op jit(solution)/shard_map/all_gather | solution.py:357
  1168.6 69.0 %all_gather.27 = bf16[262144]{0:T(1024)(128)(2,1)S(1)} all-gather(bf16[8192]{0:T(1024)(128)(2,1)S(1)} %dynamic-slice.19), channel_id=1, replica_groups=mesh['wide'=8,'narrow'=4] {'wide','narrow'}, dimensions={0}, use_global_device_ids=true | all-gather | bytes 540672 | tf_op jit(solution)/shard_map/all_gather | solution.py:366
  1243.6 4.6 reshape.505
  1248.2 4.6 reshape.507
  (310 shorter events, 157.7 us)
Async XLA Ops:
  7.2 341.4 %copy-start = (bf16[512,2048]{1,0:T(8,128)(2,1)S(1)}, bf16[512,2048]{1,0:T(8,128)(2,1)}, u32[]{:S(2)}) copy-start(bf16[512,2048]{1,0:T(8,128)(2,1)} %param.24) | copy-start | bytes 6291460
  7.2 550.1 %all-reduce.14.cloned.1.call-start = ((), (), s32[]{:S(2)}) async-start(), calls=%async_computation.3 | async-start | bytes 524288
  10.2 13.8 %copy-start.61 = (f32[512]{0:T(512)}, f32[512]{0:T(512)S(1)}, u32[]{:S(2)}) copy-start(f32[512]{0:T(512)S(1)} %convert_element_type.256) | copy-start | bytes 6148
  13.2 10.8 copy-start.63
  14.4 5.5 copy-start.49
  14.5 6.9 copy-start.52
  14.6 8.0 copy-start.54
  15.2 8.8 copy-start.65
  20.0 5.3 copy-start.70
  20.0 5.3 copy-start.69
  20.0 5.4 copy-start.71
  333.4 3.9 copy-start.2
  333.4 3.9 copy-start.59
  334.6 4.8 slice-start.4
  337.3 3.9 slice-start.5
  337.3 3.9 copy-start.40
  337.3 3.9 copy-start.42
  338.8 4.1 copy-start.45
  339.4 15.6 %copy-start.11 = (f32[512,512]{0,1:T(8,128)}, f32[512,512]{0,1:T(8,128)S(1)}, u32[]{:S(2)}) copy-start(f32[512,512]{0,1:T(8,128)S(1)} %get-tuple-element.132) | copy-start | bytes 3145732
  355.0 77.3 %copy-start.72 = (s32[256]{0:T(256)S(1)}, s32[256]{0:T(256)}, u32[]{:S(2)}) copy-start(s32[256]{0:T(256)} %param.16) | copy-start | bytes 3076
  434.2 809.4 %all-gather.3.cloned.1.call-start = ((), (), s32[]{:S(2)}) async-start(), calls=%async_computation.1 | async-start | bytes 2162688 | tf_op jit(solution)/shard_map/all_gather | solution.py:360
  565.2 5.9 copy-start.5
  565.2 5.9 copy-start.17
  583.2 4.7 copy-start.22
  588.0 6.9 slice-start
  590.5 4.4 slice-start.1
  594.9 7.3 slice-start.2
  597.2 5.1 slice-start.3
  603.7 49.2 %copy-start.27 = (bf16[8,64,512]{2,1,0:T(8,128)(2,1)}, bf16[8,64,512]{2,1,0:T(8,128)(2,1)S(1)}, u32[]{:S(2)}) copy-start(bf16[8,64,512]{2,1,0:T(8,128)(2,1)S(1)} %fusion.35) | copy-start | bytes 1572868
  627.5 4.8 copy-start.9
  627.5 4.8 copy-start.44
  627.5 6.4 copy-start.8
  627.6 6.4 copy-start.43
  632.3 3.8 copy-start.41
  636.1 3.8 copy-start.38
  636.1 5.4 copy-start.18
  637.0 4.5 copy-start.7
  637.0 4.5 copy-start.13
  642.8 4.9 copy-start.23
  664.5 8.4 copy-start.30
  664.5 8.9 copy-start.29
  678.7 16.0 %copy-start.19 = (f32[512,512]{0,1:T(8,128)}, f32[512,512]{0,1:T(8,128)S(1)}, u32[]{:S(2)}) copy-start(f32[512,512]{0,1:T(8,128)S(1)} %convolution_add_fusion.2) | copy-start | bytes 3145732
  678.7 16.0 %copy-start.33 = (bf16[8,64,512]{2,1,0:T(8,128)(2,1)S(1)}, bf16[8,64,512]{2,1,0:T(8,128)(2,1)}, u32[]{:S(2)}) copy-start(bf16[8,64,512]{2,1,0:T(8,128)(2,1)} %fusion.38) | copy-start | bytes 1572868
  696.5 233.2 %copy-start.67 = (f32[512]{0:T(512)S(1)}, f32[512]{0:T(512)}, u32[]{:S(2)}) copy-start(f32[512]{0:T(512)} %get-tuple-element.109) | copy-start | bytes 6148
  696.5 233.3 %copy-start.68 = (f32[512]{0:T(512)S(1)}, f32[512]{0:T(512)}, u32[]{:S(2)}) copy-start(f32[512]{0:T(512)} %get-tuple-element.107) | copy-start | bytes 6148
  928.1 320.1 %all-gather.5.cloned.1.call-start = ((), (), s32[]{:S(2)}) async-start(), calls=%async_computation.2 | async-start | bytes 2162688 | tf_op jit(solution)/shard_map/all_gather | solution.py:363
  943.3 295.5 %all-to-all-start = ((bf16[32,2,4096]{2,1,0:T(2,128)(2,1)}), bf16[32,2,4096]{2,1,0:T(2,128)(2,1)S(1)}, u32[]{:S(2)}, u32[]{:S(2)}) async-start(bf16[32,2,4096]{2,1,0:T(2,128)(2,1)} %reshape.522), calls=%async_computation | async-start | bytes 1048576 | tf_op jit(solution)/shard_map/all_to_all | solution.py:23
  1243.6 9.3 copy-start.1
  (35 other events, 83.5 us)
Sparse Core Ops, SparseCore 0:
  434.3 122.9 all-reduce.13
  928.3 55.8 all-gather.2
  987.1 55.8 all-gather.4
